TPU v7x, 32 devices: a 4x4x1 block of a 4x4x8 slice. The times are simulated.
32 devices in a mesh: dp: 1 (over z), heads: 4 (over y), ctx: 8 (over x, core).
Axes of the slice: x: 4, y: 4, z: 1, core: 2. Of those that a mesh axis runs over, the one named last changes fastest.
The devices are a block of a 4x4x8 slice.
Arguments:
- hidden: bfloat16 [512, 5120], P(('dp', 'ctx'))
- w_query: bfloat16 [5120, 4096], P(None, 'heads')
- w_key: bfloat16 [5120, 1024], P(None, 'heads')
- w_value: bfloat16 [5120, 1024], P(None, 'heads')
- w_out: bfloat16 [4096, 5120], P('heads')
- prefix_k: bfloat16 [8192, 8, 128], P(('dp', 'ctx'), 'heads')
- prefix_v: bfloat16 [8192, 8, 128], P(('dp', 'ctx'), 'heads')
- suffix_k: bfloat16 [512, 512, 8, 128], P(('dp', 'ctx'), None, 'heads')
- suffix_v: bfloat16 [512, 512, 8, 128], P(('dp', 'ctx'), None, 'heads')
- seq_lens: int32 [512], P(('dp', 'ctx'))
Outputs:
- output: bfloat16 [512, 5120], P(('dp', 'ctx'))
All inputs are finite; a program needn't handle non-finite values.
Results may differ from a plain program's by a relative error of at most 0.00452898.
Values are sent between devices in bfloat16 or wider.
A program may use at most 768 MiB of HBM per device.

v0:
```python
import functools
import math
import jax
import jax.numpy as jnp
from jax import lax
from jax.experimental import pallas as pl
from jax.experimental.pallas import tpu as pltpu
from jax.sharding import PartitionSpec as P

MESH = pl.DeviceIdType.MESH
F32 = jnp.float32
BF16 = jnp.bfloat16
LOW = -3.0e38
GROUP = 16
RING = 2
POS_CHUNK = 512
PIECES = 5
IN_FLIGHT = 4
VMEM_BYTES = 66000000


def dot_nt(a, b):
    return lax.dot_general(a, b, (((1,), (1,)), ((), ())), preferred_element_type=F32)


def dot_nn(a, b):
    return lax.dot_general(a, b, (((1,), (0,)), ((), ())), preferred_element_type=F32)


def pack_stats(row_max, row_sum):
    rows = row_max.shape[0]
    lane = lax.broadcasted_iota(jnp.int32, (rows, 128), 1)
    both = jnp.where(lane == 0, row_max, jnp.where(lane == 1, row_sum, 0.0))
    return jnp.transpose(both)[:8]


def unpack_stats(packed):
    rows = packed.shape[1]
    both = jnp.transpose(jnp.concatenate([packed, jnp.zeros((120, rows), F32)], axis=0))
    return both[:, 0:1], both[:, 1:2]


def merge(one, two):
    (num_a, max_a, sum_a), (num_b, max_b, sum_b) = one, two
    top = jnp.maximum(max_a, max_b)
    fac_a, fac_b = jnp.exp2(max_a - top), jnp.exp2(max_b - top)
    return num_a * fac_a + num_b * fac_b, top, sum_a * fac_a + sum_b * fac_b


def kernel(dims, hid_h, wq_h, wk_h, wv_h, wo_h, pk_h, pv_h, sk_h, sv_h, lens, out_v,
           hid, wq, wk, wv, wo, raw, flat, kpre, vpre, qg, q8, knew, vnew,
           ring_k, ring_v, qbd, sufs, sufp, scores, own_num, own_st, hold_num, hold_st, xres,
           so8, sst8, xs_num, xs_st, xr_num, xr_st, att, yhold, ys, yr, yblk,
           s_hid, s_wq, s_wkv, s_wo, s_raw, s_rawsend, s_rawrecv, s_ring, s_res, s_ress, s_resr, s_as, s_ar,
           s_qs, s_qr, s_xs, s_xr, s_xst, s_xrt, s_ys, s_yr, s_gs, s_gr):
    n_ctx, n_y, kv_n, grp = dims
    rows = hid.shape[0]
    width = hid.shape[1]
    head = kpre.shape[-1]
    heads = kv_n * grp
    local_pos = raw.shape[2] // kv_n
    scale = head ** -0.5 * math.log2(math.e)
    blk = width // n_y
    half = blk // 2
    part_rows = rows // 2
    stack = grp * part_rows

    ctx = lax.axis_index('ctx')
    ypos = lax.axis_index('heads')
    right = {'ctx': lax.rem(ctx + 2, n_ctx)}
    left = {'ctx': lax.rem(ctx + n_ctx - 2, n_ctx)}
    core = lax.rem(ctx, 2)
    partner = {'ctx': ctx + 1 - 2 * core}
    below, above = lax.rem(ypos + n_y - 1, n_y), lax.rem(ypos + 1, n_y)
    up, down = {'heads': above}, {'heads': below}
    up_cores = [{'heads': above, 'ctx': ctx - core + c} for c in range(2)]
    down_cores = [{'heads': below, 'ctx': ctx - core + c} for c in range(2)]
    up_other = {'heads': above, 'ctx': ctx + 1 - 2 * core}
    down_other = {'heads': below, 'ctx': ctx + 1 - 2 * core}
    chunks = ((0, rows // 2), (rows // 2, rows // 4), (3 * rows // 4, rows // 4))

    def remote(src, dst, send, recv, where):
        return pltpu.make_async_remote_copy(src_ref=src, dst_ref=dst, send_sem=send, recv_sem=recv,
                                            device_id=where, device_id_type=MESH)

    c_hid = pltpu.make_async_copy(hid_h, hid, s_hid)
    c_raw = [pltpu.make_async_copy(src, raw.at[0, i], s_raw.at[i]) for i, src in enumerate((pk_h, pv_h))]
    deep = width // PIECES
    c_wq = [pltpu.make_async_copy(wq_h.at[pl.ds(k * deep, deep), pl.ds(kv * grp * head, grp * head)],
                                  wq.at[kv, pl.ds(k * deep, deep), :], s_wq.at[kv, k])
            for kv in range(kv_n) for k in range(PIECES)]
    c_wkv = [pltpu.make_async_copy(src, dst, s_wkv.at[i]) for i, (src, dst) in enumerate(((wk_h, wk), (wv_h, wv)))]
    c_wo = []
    for r in range(n_y):
        col = pl.multiple_of(lax.rem(ypos + r, n_y) * blk + core * half, 128)
        c_wo.append(pltpu.make_async_copy(wo_h.at[:, pl.ds(col, half)], wo.at[r], s_wo.at[r]))
    n_groups = rows // GROUP

    def ring_copies(group):
        seqs = pl.ds(group * GROUP, GROUP)
        slot = group % RING
        return (pltpu.make_async_copy(sk_h.at[seqs], ring_k.at[slot], s_ring.at[slot, 0]),
                pltpu.make_async_copy(sv_h.at[seqs], ring_v.at[slot], s_ring.at[slot, 1]))

    def start(copies):
        for c in copies:
            c.start()

    def wait(copies):
        for c in copies:
            c.wait()

    queue = c_wq + c_raw + c_wkv

    def advance():
        if queue:
            queue.pop(0).start()

    c_hid.start()
    for _ in range(IN_FLIGHT):
        advance()

    barrier = pltpu.get_barrier_semaphore()
    for where in (partner, left, right, up, down, up_other, down_other):
        pl.semaphore_signal(barrier, inc=1, device_id=where, device_id_type=MESH)

    def deinterleave(which):
        for i, dst in enumerate((kpre, vpre)):
            flat[...] = raw[which, i].astype(F32)
            for kv in range(kv_n):
                dst[kv, pl.ds(which * local_pos, local_pos), :] = flat[pl.ds(kv, local_pos, stride=kv_n), :].astype(BF16)

    def queries(kv):
        total = None
        for k in range(PIECES):
            c_wq[kv * PIECES + k].wait()
            advance()
            at = pl.ds(k * deep, deep)
            term = dot_nn(hid[:, at], wq[kv, at, :])
            total = term if total is None else total + term
        part = total.astype(BF16)
        qg[0, kv] = part
        for g in range(grp):
            q8[pl.ds(kv * grp + g, rows, stride=heads), :] = part[:, g * head:(g + 1) * head].astype(F32)

    def send_queries(kv):
        pair = (remote(qg.at[0, kv], qg.at[1, kv], s_qs.at[0, kv], s_qr.at[1, kv], right),
                remote(qg.at[0, kv], qg.at[2, kv], s_qs.at[1, kv], s_qr.at[2, kv], left))
        start(pair)
        return pair

    c_hid.wait()
    queries(0)
    pl.semaphore_wait(barrier, 7)
    q_copies = [send_queries(0)]
    c_swap = [remote(src, raw.at[1, i], s_rawsend.at[i], s_rawrecv.at[i], partner) for i, src in enumerate((pk_h, pv_h))]
    start(c_swap)
    c_res = [pltpu.make_async_copy(hid_h.at[:, pl.ds(pl.multiple_of(ypos * blk + core * half, 128), half)], xres.at[core], s_res),
             remote(hid_h.at[:, pl.ds(pl.multiple_of(ypos * blk + (1 - core) * half, 128), half)], xres.at[core], s_ress, s_resr, partner)]
    start(c_res)
    queries(1)
    q_copies.append(send_queries(1))
    while queue:
        advance()
    wait(c_raw)
    deinterleave(0)

    wait(c_swap)
    deinterleave(1)
    start(ring_copies(0))

    n_pos = kpre.shape[1]

    n_pieces = n_pos // POS_CHUNK
    part_lanes = POS_CHUNK // 128

    def prefix_states(jobs):
        stacked, run, out = [None] * len(jobs), [None] * len(jobs), []

        def score(i, c):
            sources, kv = jobs[i]
            if c == 0:
                stacked[i] = jnp.concatenate([qg[slot, kv, pl.ds(chunk * part_rows, part_rows), pl.ds(g * head, head)]
                                              for slot, chunk in sources for g in range(grp)], axis=0)
            at = pl.ds(c * POS_CHUNK, POS_CHUNK)
            s = dot_nt(stacked[i], kpre[kv, at, :])
            scores[i % 2, :, at] = s
            for t in range(part_lanes):
                piece = s[:, t * 128:(t + 1) * 128]
                run[i] = piece if run[i] is None else jnp.maximum(run[i], piece)

        for c in range(n_pieces):
            score(0, c)
        for i, (sources, kv) in enumerate(jobs):
            row_max = jnp.max(run[i], axis=1, keepdims=True) * scale
            wide_max = jnp.broadcast_to(row_max, (2 * stack, 128))
            wide_max = jnp.concatenate([wide_max] * part_lanes, axis=1)
            total, num = None, None
            for c in range(n_pieces):
                if i + 1 < len(jobs):
                    score(i + 1, c)
                at = pl.ds(c * POS_CHUNK, POS_CHUNK)
                p = jnp.exp2(scores[i % 2, :, at] * scale - wide_max)
                for t in range(part_lanes):
                    piece = p[:, t * 128:(t + 1) * 128]
                    total = piece if total is None else total + piece
                term = dot_nn(p.astype(BF16), vpre[kv, at, :])
                num = term if num is None else num + term
            row_sum = jnp.sum(total, axis=1, keepdims=True)
            out += [(num[:stack], row_max[:stack], row_sum[:stack]), (num[stack:], row_max[stack:], row_sum[stack:])]
        return out

    sent = []

    def x_copies(i, where):
        return (remote(xs_num.at[i], xr_num.at[i], s_xs.at[i], s_xr.at[i], where),
                remote(xs_st.at[i], xr_st.at[i], s_xst.at[i], s_xrt.at[i], where))

    def post(state, i, where):
        xs_num[i] = state[0]
        xs_st[i] = pack_stats(state[1], state[2])
        out = x_copies(i, where)
        start(out)
        sent.extend(out)

    def arrived(i):
        return (xr_num[i],) + unpack_stats(xr_st[i])

    def keep(refs, i, state):
        refs[0][i] = state[0]
        lane = lax.broadcasted_iota(jnp.int32, state[0].shape, 1)
        refs[1][i] = jnp.where(lane == 0, state[1], state[2])

    def kept(refs, i):
        return refs[0][i], refs[1][i][:, 0:1], refs[1][i][:, 1:2]

    own = (own_num, own_st)
    hold = (hold_num, hold_st)

    def prefix_near(chunk):
        base = 6 * chunk
        both = ((2, chunk), (1, chunk))
        right_1, left_1, right_0, left_0 = prefix_states([(both, 1), (both, 0)])
        post(right_1, base, right)
        post(left_0, base + 1, left)
        keep(hold, 2 * chunk + 1, left_1)
        keep(hold, 2 * chunk, right_0)

    def prefix_far():
        both = ((3, 0), (3, 1))
        states = prefix_states([(both, 0), (both, 1)])
        for chunk in range(2):
            post(states[chunk], 6 * chunk + 2, right)
            post(states[2 + chunk], 6 * chunk + 3, left)

    def prefix_own():
        both = ((0, 0), (0, 1))
        for i, state in enumerate(prefix_states([(both, 0), (both, 1)])):
            keep(own, i, state)

    def relay(chunk):
        base = 6 * chunk
        for i, where in ((base + 2, right), (base + 3, left)):
            for c in x_copies(i, where):
                c.wait_recv()
        to_right, to_left = (merge(arrived(base + 2 + i), kept(hold, 2 * chunk + i)) for i in range(2))
        post(to_right, base + 4, right)
        post(to_left, base + 5, left)

    lines = GROUP * heads
    span = ring_k.shape[2]
    tile = span // 4

    def suffix_group(group):
        slot = group % RING
        lane = lax.broadcasted_iota(jnp.int32, (head, lines), 1)
        q_t = jnp.transpose(q8[pl.ds(group * lines, lines), :])
        for j in range(GROUP // 2):
            both = [jnp.where(lane // heads == 2 * j + e, q_t, 0.0) for e in range(2)]
            qbd[j] = jnp.concatenate(both, axis=0).astype(BF16)
        one = lax.broadcasted_iota(jnp.int32, (1, lines), 1)
        length = jnp.zeros((1, lines), jnp.int32)
        for b in range(GROUP):
            length = jnp.where(one // heads == b, lens[group * GROUP + b], length)
        line = lax.broadcasted_iota(jnp.int32, (tile, lines), 0)
        lane = lax.broadcasted_iota(jnp.int32, (tile, lines), 1)
        mine = lax.rem(line, kv_n) == lax.rem(lane, heads) // grp
        place = jnp.where(mine, line // kv_n, span)
        wait(ring_copies(group))
        run = jnp.full((1, lines), LOW, F32)
        for c in range(4):
            at = pl.ds(c * tile, tile)
            s = None
            for j in range(GROUP // 2):
                keys = jnp.concatenate([ring_k[slot, 2 * j, at, :], ring_k[slot, 2 * j + 1, at, :]], axis=1)
                term = dot_nn(keys, qbd[j])
                s = term if s is None else s + term
            s = jnp.where(place < length - c * (tile // kv_n), s * scale, -jnp.inf)
            sufs[at, :] = s
            run = jnp.maximum(run, jnp.max(s, axis=0, keepdims=True))
        total = jnp.zeros((1, lines), F32)
        for c in range(4):
            p = jnp.exp2(sufs[pl.ds(c * tile, tile), :] - run)
            total = total + jnp.sum(p, axis=0, keepdims=True)
            sufp[:, pl.ds(c * tile, tile)] = jnp.transpose(p).astype(BF16)
        stats = jnp.concatenate([run, total, jnp.zeros((head - 2, lines), F32)], axis=0)
        sst8[pl.ds(group * lines, lines), :] = jnp.transpose(stats)
        for j in range(GROUP // 2):
            weights = sufp[pl.ds(2 * j * heads, 2 * heads), :]
            for e in range(2):
                o = dot_nn(weights, ring_v[slot, 2 * j + e])
                so8[pl.ds(group * lines + (2 * j + e) * heads, heads), :] = o[e * heads:(e + 1) * heads]
        if group + RING < n_groups:
            start(ring_copies(group + RING))

    def merge_prefix(chunk):
        base = 6 * chunk
        for i, where in ((base + 1, left), (base + 4, right), (base, right), (base + 5, left)):
            for c in x_copies(i, where):
                c.wait_recv()
        merged = [functools.reduce(merge, [kept(own, chunk), arrived(base + 1), arrived(base + 4)]),
                  functools.reduce(merge, [kept(own, 2 + chunk), arrived(base), arrived(base + 5)])]
        for kv in range(kv_n):
            keep(own, 2 * kv + chunk, merged[kv])

    def att_copy(chunk):
        first, n = chunks[chunk]
        ref = att.at[core, pl.ds(first, n), :]
        return remote(ref, ref, s_as.at[chunk], s_ar.at[chunk], partner)

    def combine(chunk):
        first, n = chunks[chunk]
        at_rows = pl.ds(first, n)
        which, off = first // part_rows, first % part_rows
        for kv in range(kv_n):
            rest = []
            for g in range(grp):
                every = pl.ds(first * heads + kv * grp + g, n, stride=heads)
                stats = sst8[every, :]
                pre_at = pl.ds(g * part_rows + off, n)
                pre = own_st[2 * kv + which, pre_at, :]
                rest.append((so8[every, :], stats[:, 0:1], stats[:, 1:2], q8[every, :],
                             own_num[2 * kv + which, pre_at, :], pre[:, 0:1], pre[:, 1:2]))
            num, top, tot, qs, pre_num, pre_top, pre_tot = (jnp.concatenate(list(v), axis=0) for v in zip(*rest))
            state = merge((pre_num, pre_top, pre_tot), (num, top, tot))
            kn = jnp.concatenate([knew[at_rows, pl.ds(kv * head, head)]] * grp, axis=0)
            vn = jnp.concatenate([vnew[at_rows, pl.ds(kv * head, head)]] * grp, axis=0)
            s_new = jnp.sum(qs * kn, axis=1, keepdims=True) * scale
            state = merge(state, (vn, s_new, jnp.ones_like(s_new)))
            res = (state[0] / state[2]).astype(BF16)
            for g in range(grp):
                att[core, at_rows, pl.ds((kv * grp + g) * head, head)] = res[g * n:(g + 1) * n]
        c = att_copy(chunk)
        c.start()
        sent.append(c)

    ysent = []

    def y_copy(chunk, i, where):
        at = pl.ds(0, chunks[chunk][1])
        return remote(ys.at[i, at], yr.at[i, at], s_ys.at[i], s_yr.at[i], where)

    def y_post(chunk, val, i, where):
        ys[i, :val.shape[0]] = val
        c = y_copy(chunk, i, where)
        c.start()
        ysent.append(c)

    def project(chunk):
        base = 6 * chunk
        first, n = chunks[chunk]
        att_copy(chunk).wait_recv()
        both = jnp.concatenate([att[c, pl.ds(first, n), :] for c in range(2)], axis=0)

        def y_part(r):
            if chunk == 0:
                c_wo[r].wait()
            val = dot_nn(both, wo[r])
            return val[:n], val[n:]

        one, two = y_part(n_y // 2)
        y_post(chunk, one, base, up)
        y_post(chunk, two, base + 1, down)
        one, two = y_part(1)
        y_post(chunk, two, base + 2, up)
        yhold[chunk, 0, :n] = one
        one, two = y_part(n_y - 1)
        y_post(chunk, one, base + 3, down)
        yhold[chunk, 1, :n] = two
        one, two = y_part(0)
        yhold[chunk, 2, :n] = one
        yhold[chunk, 3, :n] = two

    def y_relay(chunk):
        base = 6 * chunk
        n = chunks[chunk][1]
        y_copy(chunk, base, up).wait_recv()
        y_post(chunk, yhold[chunk, 0, :n] + yr[base, :n], base + 4, up)
        y_copy(chunk, base + 1, down).wait_recv()
        y_post(chunk, yhold[chunk, 1, :n] + yr[base + 1, :n], base + 5, down)

    gsend = []

    def region(chunk, dest, which):
        first, n = chunks[chunk]
        return out_v.at[pl.ds(first, n), pl.ds(pl.multiple_of(dest * blk + which * half, 128), half)]

    def g_start(src, dst, chunk, slot, which, sem, where):
        c = remote(src, dst, s_gs.at[chunk, sem], s_gr.at[chunk, slot, which], where)
        c.start()
        gsend.append(c)

    def g_wait(chunk, slot, which):
        ref = region(chunk, ypos, 0)
        remote(ref, ref, s_gs.at[chunk, 0], s_gr.at[chunk, slot, which], up).wait_recv()

    def finish(chunk):
        base = 6 * chunk
        first, n = chunks[chunk]
        mine = region(chunk, ypos, core)
        done = []
        for c, (near, merged) in enumerate(((base + 3, base + 4), (base + 2, base + 5))):
            val = yhold[chunk, 2 + c, :n]
            for i in (near, merged):
                y_copy(chunk, i, up if i % 2 == 0 else down).wait_recv()
                val = val + yr[i, :n]
            val = (val + xres[c, pl.ds(first, n), :].astype(F32)).astype(BF16)
            yblk[chunk, c, :n] = val
            src = yblk.at[chunk, c, pl.ds(0, n)]
            order = ((0, up_cores[c]), (1, down_cores[c]))
            for slot, where in (order if c == 0 else order[::-1]):
                g_start(src, mine, chunk, slot, core, 2 * c + slot, where)
            done.append(val)
        col = pl.multiple_of(ypos * blk + core * half, 128)
        out_v[pl.ds(first, n), pl.ds(col, half)] = jnp.where(core == 0, done[0], done[1])
        g_start(yblk.at[chunk, 1 - core, pl.ds(0, n)], mine, chunk, 3, core, 4, partner)

    def forward(chunk):
        g_wait(chunk, 0, 0)
        ref = region(chunk, below, 0)
        g_start(ref, ref, chunk, 2, 0, 5, up)
        g_wait(chunk, 1, 1)
        ref = region(chunk, above, 1)
        g_start(ref, ref, chunk, 2, 1, 6, down)

    def collect(chunk):
        g_wait(chunk, 0, 1)
        g_wait(chunk, 1, 0)
        g_wait(chunk, 3, 1 - core)
        g_wait(chunk, 2, 0)
        g_wait(chunk, 2, 1)

    prefix_own()
    q_copies[0][0].wait_recv()
    fwd_right = remote(qg.at[1, 0], qg.at[3, 0], s_qs.at[2, 0], s_qr.at[3, 0], right)
    fwd_right.start()
    wait(c_wkv)
    start(ring_copies(1))
    for r in (n_y // 2, 1, n_y - 1, 0):
        c_wo[r].start()
    knew[...] = dot_nn(hid[...], wk[...]).astype(BF16).astype(F32)
    vnew[...] = dot_nn(hid[...], wv[...]).astype(BF16).astype(F32)
    q_copies[1][1].wait_recv()
    fwd_left = remote(qg.at[2, 1], qg.at[3, 1], s_qs.at[2, 1], s_qr.at[3, 1], left)
    fwd_left.start()
    q_copies[1][0].wait_recv()
    q_copies[0][1].wait_recv()
    prefix_near(0)
    prefix_near(1)
    fwd_right.wait_recv()
    fwd_left.wait_recv()
    prefix_far()

    suffix_group(0)
    suffix_group(1)
    relay(0)
    relay(1)
    for group in range(2, n_groups):
        suffix_group(group)
    merge_prefix(0)
    combine(0)
    merge_prefix(1)
    combine(1)
    wait(c_res)
    project(0)
    combine(2)
    project(1)
    project(2)
    y_relay(0)
    y_relay(1)
    for c in [fwd_right, fwd_left] + sent:
        c.wait_send()
    for pair in q_copies:
        for c in pair:
            c.wait_send()
    y_relay(2)
    finish(0)
    finish(1)
    finish(2)
    for c in ysent:
        c.wait_send()
    forward(0)
    forward(1)
    forward(2)
    late = gsend[-2:]
    for c in gsend[:-2]:
        c.wait_send()
    collect(0)
    collect(1)
    collect(2)
    for c in late:
        c.wait_send()


def store(src, dst, sem):
    c = pltpu.make_async_copy(src, dst, sem)
    c.start()
    c.wait()


def solution(mesh):
    n_ctx, n_y = mesh.shape['ctx'], mesh.shape['heads']
    row_spec = P(('dp', 'ctx'), None)
    col_spec = P(None, 'heads')
    pre_spec = P(('dp', 'ctx'), 'heads', None)
    suf_spec = P(('dp', 'ctx'), None, 'heads', None)

    def local_step(hidden, w_query, w_key, w_value, w_out, prefix_k, prefix_v, suffix_k, suffix_v, seq_lens):
        rows, width = hidden.shape
        pos, kv_n, head = prefix_k.shape
        slots = suffix_k.shape[1]
        grp = w_query.shape[1] // (kv_n * head)
        heads = kv_n * grp
        blk = width // n_y
        half_rows = rows // 2
        stack = grp * half_rows
        lines = GROUP * heads
        dma = pltpu.SemaphoreType.DMA
        scratch = dict(
            hid=pltpu.VMEM((rows, width), BF16),
            wq=pltpu.VMEM((kv_n, width, grp * head), BF16),
            wk=pltpu.VMEM((width, kv_n * head), BF16),
            wv=pltpu.VMEM((width, kv_n * head), BF16),
            wo=pltpu.VMEM((n_y, heads * head, blk // 2), BF16),
            raw=pltpu.VMEM((2, 2, pos * kv_n, head), BF16),
            flat=pltpu.VMEM((pos * kv_n, head), F32),
            kpre=pltpu.VMEM((kv_n, 2 * pos, head), BF16),
            vpre=pltpu.VMEM((kv_n, 2 * pos, head), BF16),
            qg=pltpu.VMEM((4, kv_n, rows, grp * head), BF16),
            q8=pltpu.VMEM((rows * heads, head), F32),
            knew=pltpu.VMEM((rows, kv_n * head), F32),
            vnew=pltpu.VMEM((rows, kv_n * head), F32),
            ring_k=pltpu.VMEM((RING, GROUP, slots * kv_n, head), BF16),
            ring_v=pltpu.VMEM((RING, GROUP, slots * kv_n, head), BF16),
            qbd=pltpu.VMEM((GROUP // 2, 2 * head, lines), BF16),
            sufs=pltpu.VMEM((slots * kv_n, lines), F32),
            sufp=pltpu.VMEM((lines, slots * kv_n), BF16),
            scores=pltpu.VMEM((2, 2 * stack, 2 * pos), F32),
            own_num=pltpu.VMEM((2 * kv_n, stack, head), F32),
            own_st=pltpu.VMEM((2 * kv_n, stack, 128), F32),
            hold_num=pltpu.VMEM((4, stack, head), F32),
            hold_st=pltpu.VMEM((4, stack, 128), F32),
            xres=pltpu.VMEM((2, rows, blk // 2), BF16),
            so8=pltpu.VMEM((rows * heads, head), F32),
            sst8=pltpu.VMEM((rows * heads, head), F32),
            xs_num=pltpu.VMEM((12, stack, head), F32),
            xs_st=pltpu.VMEM((12, 8, stack), F32),
            xr_num=pltpu.VMEM((12, stack, head), F32),
            xr_st=pltpu.VMEM((12, 8, stack), F32),
            att=pltpu.VMEM((2, rows, heads * head), BF16),
            yhold=pltpu.VMEM((3, 4, half_rows, blk // 2), F32),
            ys=pltpu.VMEM((18, half_rows, blk // 2), F32),
            yr=pltpu.VMEM((18, half_rows, blk // 2), F32),
            yblk=pltpu.VMEM((3, 2, half_rows, blk // 2), BF16),
            s_hid=dma(()), s_wq=dma((kv_n, PIECES)), s_wkv=dma((2,)), s_wo=dma((n_y,)),
            s_raw=dma((2,)), s_rawsend=dma((2,)), s_rawrecv=dma((2,)), s_ring=dma((RING, 2)),
            s_res=dma(()), s_ress=dma(()), s_resr=dma(()), s_as=dma((3,)), s_ar=dma((3,)),
            s_qs=dma((3, kv_n)), s_qr=dma((4, kv_n)),
            s_xs=dma((12,)), s_xr=dma((12,)), s_xst=dma((12,)), s_xrt=dma((12,)),
            s_ys=dma((18,)), s_yr=dma((18,)), s_gs=dma((3, 7)), s_gr=dma((3, 4, 2)),
        )
        hbm = pl.BlockSpec(memory_space=pl.ANY)
        out = pl.pallas_call(
            functools.partial(kernel, (n_ctx, n_y, kv_n, grp)),
            out_shape=pltpu.VMEM((rows, width), BF16),
            in_specs=[hbm] * 9 + [pl.BlockSpec(memory_space=pltpu.SMEM)],
            out_specs=pl.BlockSpec(memory_space=pltpu.VMEM),
            scratch_shapes=list(scratch.values()),
            compiler_params=pltpu.CompilerParams(collective_id=0, has_side_effects=True, vmem_limit_bytes=VMEM_BYTES),
        )(hidden, w_query, w_key, w_value, w_out,
          prefix_k.reshape(pos * kv_n, head), prefix_v.reshape(pos * kv_n, head),
          suffix_k.reshape(rows, slots * kv_n, head), suffix_v.reshape(rows, slots * kv_n, head), seq_lens)
        return pl.pallas_call(
            store,
            out_shape=jax.ShapeDtypeStruct((rows, width), BF16),
            in_specs=[pl.BlockSpec(memory_space=pltpu.VMEM)],
            out_specs=hbm,
            scratch_shapes=[dma(())],
            compiler_params=pltpu.CompilerParams(vmem_limit_bytes=1048576),
        )(out)

    return jax.shard_map(local_step, mesh=mesh, in_specs=(row_spec, col_spec, col_spec, col_spec, P('heads', None), pre_spec, pre_spec, suf_spec, suf_spec, P(('dp', 'ctx'))), out_specs=row_spec, check_vma=False)
```

profile of v0, /device:TPU:97, one launch (start us, length us, event | category | flops | bytes accessed | tf_op | source)
XLA Modules:
  0.0 55.9 jit_solution(2379441820637129282)
XLA Ops:
  0.0 54.9 %shard_map.100.src = bf16[64,5120]{1,0:T(8,128)(2,1)S(1)} custom-call(bf16[64,5120]{1,0:T(8,128)(2,1)} %hid_h.1, bf16[5120,1024]{1,0:T(8,128)(2,1)} %wq_h.1, bf16[5120,256]{1,0:T(8,128)(2,1)} %wk_h.1, bf16[5120,256]{1,0:T(8,128)(2,1)} %wv_h.1, bf16[1024,5120]{1,0:T(8,128)(2,1)} %wo_h.1, bf16[2048,128]{1,0:T(8,128)(2,1)} %bitcast.6, ...), custom_call_target="tpu_custom_call" | custom-call | tf_op jit(solution)/shard_map/pallas_call | solution.py:583
  54.9 0.8 %shard_map.101 = bf16[64,5120]{1,0:T(8,128)(2,1)} custom-call(bf16[64,5120]{1,0:T(8,128)(2,1)S(1)} %shard_map.100.src), custom_call_target="tpu_custom_call" | custom-call | tf_op jit(solution)/shard_map/pallas_call | solution.py:593
where the time goes:
time: 56 us; the launch traced here: 55.9 us
  Pallas kernels  55.8 us (100%)
    pallas_call x1, Pallas kernels, local_step(): pl.pallas_call(functools.partial(kernel, (n_ctx, n_y, kv_n, grp)), out_sh...  54.9 us

commit v1 on v0

--- a/solution.py
+++ b/solution.py
@@ -15,7 +15,7 @@
 RING = 2
 POS_CHUNK = 512
 PIECES = 5
-IN_FLIGHT = 4
+IN_FLIGHT = 6
 VMEM_BYTES = 66000000
 
 
@@ -49,10 +49,10 @@
 
 def kernel(dims, hid_h, wq_h, wk_h, wv_h, wo_h, pk_h, pv_h, sk_h, sv_h, lens, out_v,
            hid, wq, wk, wv, wo, raw, flat, kpre, vpre, qg, q8, knew, vnew,
-           ring_k, ring_v, qbd, sufs, sufp, scores, own_num, own_st, hold_num, hold_st, xres,
-           so8, sst8, xs_num, xs_st, xr_num, xr_st, att, yhold, ys, yr, yblk,
+           ring, qbd, sufs, sufp, scores, own_num, own_st, hold_num, hold_st, xres,
+           so8, sst8, xs, xr, att, yhold, ys, yr, yblk,
            s_hid, s_wq, s_wkv, s_wo, s_raw, s_rawsend, s_rawrecv, s_ring, s_res, s_ress, s_resr, s_as, s_ar,
-           s_qs, s_qr, s_xs, s_xr, s_xst, s_xrt, s_ys, s_yr, s_gs, s_gr):
+           s_qs, s_qr, s_xs, s_xr, s_ys, s_yr, s_gs, s_gr, s_gl):
     n_ctx, n_y, kv_n, grp = dims
     rows = hid.shape[0]
     width = hid.shape[1]
@@ -84,10 +84,10 @@
                                             device_id=where, device_id_type=MESH)
 
     c_hid = pltpu.make_async_copy(hid_h, hid, s_hid)
-    c_raw = [pltpu.make_async_copy(src, raw.at[0, i], s_raw.at[i]) for i, src in enumerate((pk_h, pv_h))]
+    c_raw = [pltpu.make_async_copy(src, raw.at[0, i], s_raw) for i, src in enumerate((pk_h, pv_h))]
     deep = width // PIECES
     c_wq = [pltpu.make_async_copy(wq_h.at[pl.ds(k * deep, deep), pl.ds(kv * grp * head, grp * head)],
-                                  wq.at[kv, pl.ds(k * deep, deep), :], s_wq.at[kv, k])
+                                  wq.at[kv, pl.ds(k * deep, deep), :], s_wq.at[(kv * PIECES + k) % (IN_FLIGHT + 1)])
             for kv in range(kv_n) for k in range(PIECES)]
     c_wkv = [pltpu.make_async_copy(src, dst, s_wkv.at[i]) for i, (src, dst) in enumerate(((wk_h, wk), (wv_h, wv)))]
     c_wo = []
@@ -99,8 +99,7 @@
     def ring_copies(group):
         seqs = pl.ds(group * GROUP, GROUP)
         slot = group % RING
-        return (pltpu.make_async_copy(sk_h.at[seqs], ring_k.at[slot], s_ring.at[slot, 0]),
-                pltpu.make_async_copy(sv_h.at[seqs], ring_v.at[slot], s_ring.at[slot, 1]))
+        return [pltpu.make_async_copy(src.at[seqs], ring.at[slot, i], s_ring.at[slot]) for i, src in enumerate((sk_h, sv_h))]
 
     def start(copies):
         for c in copies:
@@ -144,8 +143,8 @@
             q8[pl.ds(kv * grp + g, rows, stride=heads), :] = part[:, g * head:(g + 1) * head].astype(F32)
 
     def send_queries(kv):
-        pair = (remote(qg.at[0, kv], qg.at[1, kv], s_qs.at[0, kv], s_qr.at[1, kv], right),
-                remote(qg.at[0, kv], qg.at[2, kv], s_qs.at[1, kv], s_qr.at[2, kv], left))
+        pair = (remote(qg.at[0, kv], qg.at[1, kv], s_qs, s_qr.at[0, kv], right),
+                remote(qg.at[0, kv], qg.at[2, kv], s_qs, s_qr.at[1, kv], left))
         start(pair)
         return pair
 
@@ -153,7 +152,7 @@
     queries(0)
     pl.semaphore_wait(barrier, 7)
     q_copies = [send_queries(0)]
-    c_swap = [remote(src, raw.at[1, i], s_rawsend.at[i], s_rawrecv.at[i], partner) for i, src in enumerate((pk_h, pv_h))]
+    c_swap = [remote(src, raw.at[1, i], s_rawsend, s_rawrecv, partner) for i, src in enumerate((pk_h, pv_h))]
     start(c_swap)
     c_res = [pltpu.make_async_copy(hid_h.at[:, pl.ds(pl.multiple_of(ypos * blk + core * half, 128), half)], xres.at[core], s_res),
              remote(hid_h.at[:, pl.ds(pl.multiple_of(ypos * blk + (1 - core) * half, 128), half)], xres.at[core], s_ress, s_resr, partner)]
@@ -162,10 +161,10 @@
     q_copies.append(send_queries(1))
     while queue:
         advance()
-    wait(c_raw)
+    pltpu.make_async_copy(raw.at[0], raw.at[0], s_raw).wait()
     deinterleave(0)
 
-    wait(c_swap)
+    remote(raw.at[1], raw.at[1], s_rawsend, s_rawrecv, partner).wait()
     deinterleave(1)
     start(ring_copies(0))
 
@@ -210,21 +209,16 @@
             out += [(num[:stack], row_max[:stack], row_sum[:stack]), (num[stack:], row_max[stack:], row_sum[stack:])]
         return out
 
-    sent = []
-
     def x_copies(i, where):
-        return (remote(xs_num.at[i], xr_num.at[i], s_xs.at[i], s_xr.at[i], where),
-                remote(xs_st.at[i], xr_st.at[i], s_xst.at[i], s_xrt.at[i], where))
+        return remote(xs.at[i], xr.at[i], s_xs, s_xr.at[i], where)
 
     def post(state, i, where):
-        xs_num[i] = state[0]
-        xs_st[i] = pack_stats(state[1], state[2])
-        out = x_copies(i, where)
-        start(out)
-        sent.extend(out)
+        xs[i, :stack] = state[0]
+        xs[i, stack:, :stack] = pack_stats(state[1], state[2])
+        x_copies(i, where).start()
 
     def arrived(i):
-        return (xr_num[i],) + unpack_stats(xr_st[i])
+        return (xr[i, :stack],) + unpack_stats(xr[i, stack:, :stack])
 
     def keep(refs, i, state):
         refs[0][i] = state[0]
@@ -261,14 +255,13 @@
     def relay(chunk):
         base = 6 * chunk
         for i, where in ((base + 2, right), (base + 3, left)):
-            for c in x_copies(i, where):
-                c.wait_recv()
+            x_copies(i, where).wait_recv()
         to_right, to_left = (merge(arrived(base + 2 + i), kept(hold, 2 * chunk + i)) for i in range(2))
         post(to_right, base + 4, right)
         post(to_left, base + 5, left)
 
     lines = GROUP * heads
-    span = ring_k.shape[2]
+    span = ring.shape[3]
     tile = span // 4
 
     def suffix_group(group):
@@ -286,13 +279,13 @@
         lane = lax.broadcasted_iota(jnp.int32, (tile, lines), 1)
         mine = lax.rem(line, kv_n) == lax.rem(lane, heads) // grp
         place = jnp.where(mine, line // kv_n, span)
-        wait(ring_copies(group))
+        pltpu.make_async_copy(ring.at[slot], ring.at[slot], s_ring.at[slot]).wait()
         run = jnp.full((1, lines), LOW, F32)
         for c in range(4):
             at = pl.ds(c * tile, tile)
             s = None
             for j in range(GROUP // 2):
-                keys = jnp.concatenate([ring_k[slot, 2 * j, at, :], ring_k[slot, 2 * j + 1, at, :]], axis=1)
+                keys = jnp.concatenate([ring[slot, 0, 2 * j, at, :], ring[slot, 0, 2 * j + 1, at, :]], axis=1)
                 term = dot_nn(keys, qbd[j])
                 s = term if s is None else s + term
             s = jnp.where(place < length - c * (tile // kv_n), s * scale, -jnp.inf)
@@ -308,7 +301,7 @@
         for j in range(GROUP // 2):
             weights = sufp[pl.ds(2 * j * heads, 2 * heads), :]
             for e in range(2):
-                o = dot_nn(weights, ring_v[slot, 2 * j + e])
+                o = dot_nn(weights, ring[slot, 1, 2 * j + e])
                 so8[pl.ds(group * lines + (2 * j + e) * heads, heads), :] = o[e * heads:(e + 1) * heads]
         if group + RING < n_groups:
             start(ring_copies(group + RING))
@@ -316,8 +309,7 @@
     def merge_prefix(chunk):
         base = 6 * chunk
         for i, where in ((base + 1, left), (base + 4, right), (base, right), (base + 5, left)):
-            for c in x_copies(i, where):
-                c.wait_recv()
+            x_copies(i, where).wait_recv()
         merged = [functools.reduce(merge, [kept(own, chunk), arrived(base + 1), arrived(base + 4)]),
                   functools.reduce(merge, [kept(own, 2 + chunk), arrived(base), arrived(base + 5)])]
         for kv in range(kv_n):
@@ -326,7 +318,7 @@
     def att_copy(chunk):
         first, n = chunks[chunk]
         ref = att.at[core, pl.ds(first, n), :]
-        return remote(ref, ref, s_as.at[chunk], s_ar.at[chunk], partner)
+        return remote(ref, ref, s_as, s_ar.at[chunk], partner)
 
     def combine(chunk):
         first, n = chunks[chunk]
@@ -350,21 +342,15 @@
             res = (state[0] / state[2]).astype(BF16)
             for g in range(grp):
                 att[core, at_rows, pl.ds((kv * grp + g) * head, head)] = res[g * n:(g + 1) * n]
-        c = att_copy(chunk)
-        c.start()
-        sent.append(c)
-
-    ysent = []
+        att_copy(chunk).start()
 
     def y_copy(chunk, i, where):
         at = pl.ds(0, chunks[chunk][1])
-        return remote(ys.at[i, at], yr.at[i, at], s_ys.at[i], s_yr.at[i], where)
+        return remote(ys.at[i, at], yr.at[i, at], s_ys, s_yr.at[i], where)
 
     def y_post(chunk, val, i, where):
         ys[i, :val.shape[0]] = val
-        c = y_copy(chunk, i, where)
-        c.start()
-        ysent.append(c)
+        y_copy(chunk, i, where).start()
 
     def project(chunk):
         base = 6 * chunk
@@ -399,20 +385,25 @@
         y_copy(chunk, base + 1, down).wait_recv()
         y_post(chunk, yhold[chunk, 1, :n] + yr[base + 1, :n], base + 5, down)
 
-    gsend = []
-
     def region(chunk, dest, which):
         first, n = chunks[chunk]
         return out_v.at[pl.ds(first, n), pl.ds(pl.multiple_of(dest * blk + which * half, 128), half)]
 
-    def g_start(src, dst, chunk, slot, which, sem, where):
-        c = remote(src, dst, s_gs.at[chunk, sem], s_gr.at[chunk, slot, which], where)
-        c.start()
-        gsend.append(c)
-
-    def g_wait(chunk, slot, which):
+    def g_start(src, dst, sem, where):
+        remote(src, dst, s_gs, sem, where).start()
+
+    def g_wait(chunk, slot):
         ref = region(chunk, ypos, 0)
-        remote(ref, ref, s_gs.at[chunk, 0], s_gr.at[chunk, slot, which], up).wait_recv()
+        remote(ref, ref, s_gs, s_gr.at[chunk, slot], up).wait_recv()
+
+    def g_first(src, dst, chunk, slot, where):
+        @pl.when(core == slot)
+        def _():
+            g_start(src, dst, s_gr.at[chunk, slot], where)
+
+        @pl.when(core != slot)
+        def _():
+            g_start(src, dst, s_gl, where)
 
     def finish(chunk):
         base = 6 * chunk
@@ -427,32 +418,28 @@
             val = (val + xres[c, pl.ds(first, n), :].astype(F32)).astype(BF16)
             yblk[chunk, c, :n] = val
             src = yblk.at[chunk, c, pl.ds(0, n)]
-            order = ((0, up_cores[c]), (1, down_cores[c]))
-            for slot, where in (order if c == 0 else order[::-1]):
-                g_start(src, mine, chunk, slot, core, 2 * c + slot, where)
+            if c == 0:
+                g_first(src, mine, chunk, 0, up_cores[c])
+                g_first(src, mine, chunk, 1, down_cores[c])
+            else:
+                g_first(src, mine, chunk, 1, down_cores[c])
+                g_first(src, mine, chunk, 0, up_cores[c])
             done.append(val)
         col = pl.multiple_of(ypos * blk + core * half, 128)
         out_v[pl.ds(first, n), pl.ds(col, half)] = jnp.where(core == 0, done[0], done[1])
-        g_start(yblk.at[chunk, 1 - core, pl.ds(0, n)], mine, chunk, 3, core, 4, partner)
+        g_start(yblk.at[chunk, 1 - core, pl.ds(0, n)], mine, s_gl, partner)
 
     def forward(chunk):
-        g_wait(chunk, 0, 0)
+        g_wait(chunk, 0)
         ref = region(chunk, below, 0)
-        g_start(ref, ref, chunk, 2, 0, 5, up)
-        g_wait(chunk, 1, 1)
+        g_start(ref, ref, s_gl, up)
+        g_wait(chunk, 1)
         ref = region(chunk, above, 1)
-        g_start(ref, ref, chunk, 2, 1, 6, down)
-
-    def collect(chunk):
-        g_wait(chunk, 0, 1)
-        g_wait(chunk, 1, 0)
-        g_wait(chunk, 3, 1 - core)
-        g_wait(chunk, 2, 0)
-        g_wait(chunk, 2, 1)
+        g_start(ref, ref, s_gl, down)
 
     prefix_own()
     q_copies[0][0].wait_recv()
-    fwd_right = remote(qg.at[1, 0], qg.at[3, 0], s_qs.at[2, 0], s_qr.at[3, 0], right)
+    fwd_right = remote(qg.at[1, 0], qg.at[3, 0], s_qs, s_qr.at[2, 0], right)
     fwd_right.start()
     wait(c_wkv)
     start(ring_copies(1))
@@ -461,7 +448,7 @@
     knew[...] = dot_nn(hid[...], wk[...]).astype(BF16).astype(F32)
     vnew[...] = dot_nn(hid[...], wv[...]).astype(BF16).astype(F32)
     q_copies[1][1].wait_recv()
-    fwd_left = remote(qg.at[2, 1], qg.at[3, 1], s_qs.at[2, 1], s_qr.at[3, 1], left)
+    fwd_left = remote(qg.at[2, 1], qg.at[3, 1], s_qs, s_qr.at[2, 1], left)
     fwd_left.start()
     q_copies[1][0].wait_recv()
     q_copies[0][1].wait_recv()
@@ -475,41 +462,34 @@
     suffix_group(1)
     relay(0)
     relay(1)
-    for group in range(2, n_groups):
-        suffix_group(group)
+    suffix_group(2)
     merge_prefix(0)
     combine(0)
+    wait(c_res)
     merge_prefix(1)
+    project(0)
+    for group in range(3, n_groups):
+        suffix_group(group)
     combine(1)
-    wait(c_res)
-    project(0)
     combine(2)
+    y_relay(0)
     project(1)
     project(2)
-    y_relay(0)
     y_relay(1)
-    for c in [fwd_right, fwd_left] + sent:
-        c.wait_send()
-    for pair in q_copies:
-        for c in pair:
-            c.wait_send()
     y_relay(2)
     finish(0)
     finish(1)
     finish(2)
-    for c in ysent:
-        c.wait_send()
+    remote(qg.at[pl.ds(0, 3)], qg.at[pl.ds(0, 3)], s_qs, s_qr.at[0, 0], right).wait_send()
+    remote(xs, xr, s_xs, s_xr.at[0], right).wait_send()
+    remote(att.at[0], att.at[0], s_as, s_ar.at[0], partner).wait_send()
+    y_all = pl.ds(0, 12)
+    remote(ys.at[y_all], yr.at[y_all], s_ys, s_yr.at[0], up).wait_send()
     forward(0)
     forward(1)
     forward(2)
-    late = gsend[-2:]
-    for c in gsend[:-2]:
-        c.wait_send()
-    collect(0)
-    collect(1)
-    collect(2)
-    for c in late:
-        c.wait_send()
+    remote(yr.at[pl.ds(0, 5)], yr.at[pl.ds(0, 5)], s_gs, s_gl, up).wait_recv()
+    remote(ys.at[pl.ds(0, 7)], yr.at[pl.ds(0, 7)], s_gs, s_gl, up).wait_send()
 
 
 def store(src, dst, sem):
@@ -550,8 +530,7 @@
             q8=pltpu.VMEM((rows * heads, head), F32),
             knew=pltpu.VMEM((rows, kv_n * head), F32),
             vnew=pltpu.VMEM((rows, kv_n * head), F32),
-            ring_k=pltpu.VMEM((RING, GROUP, slots * kv_n, head), BF16),
-            ring_v=pltpu.VMEM((RING, GROUP, slots * kv_n, head), BF16),
+            ring=pltpu.VMEM((RING, 2, GROUP, slots * kv_n, head), BF16),
             qbd=pltpu.VMEM((GROUP // 2, 2 * head, lines), BF16),
             sufs=pltpu.VMEM((slots * kv_n, lines), F32),
             sufp=pltpu.VMEM((lines, slots * kv_n), BF16),
@@ -563,21 +542,19 @@
             xres=pltpu.VMEM((2, rows, blk // 2), BF16),
             so8=pltpu.VMEM((rows * heads, head), F32),
             sst8=pltpu.VMEM((rows * heads, head), F32),
-            xs_num=pltpu.VMEM((12, stack, head), F32),
-            xs_st=pltpu.VMEM((12, 8, stack), F32),
-            xr_num=pltpu.VMEM((12, stack, head), F32),
-            xr_st=pltpu.VMEM((12, 8, stack), F32),
+            xs=pltpu.VMEM((12, stack + 8, head), F32),
+            xr=pltpu.VMEM((12, stack + 8, head), F32),
             att=pltpu.VMEM((2, rows, heads * head), BF16),
             yhold=pltpu.VMEM((3, 4, half_rows, blk // 2), F32),
             ys=pltpu.VMEM((18, half_rows, blk // 2), F32),
             yr=pltpu.VMEM((18, half_rows, blk // 2), F32),
             yblk=pltpu.VMEM((3, 2, half_rows, blk // 2), BF16),
-            s_hid=dma(()), s_wq=dma((kv_n, PIECES)), s_wkv=dma((2,)), s_wo=dma((n_y,)),
-            s_raw=dma((2,)), s_rawsend=dma((2,)), s_rawrecv=dma((2,)), s_ring=dma((RING, 2)),
-            s_res=dma(()), s_ress=dma(()), s_resr=dma(()), s_as=dma((3,)), s_ar=dma((3,)),
-            s_qs=dma((3, kv_n)), s_qr=dma((4, kv_n)),
-            s_xs=dma((12,)), s_xr=dma((12,)), s_xst=dma((12,)), s_xrt=dma((12,)),
-            s_ys=dma((18,)), s_yr=dma((18,)), s_gs=dma((3, 7)), s_gr=dma((3, 4, 2)),
+            s_hid=dma(()), s_wq=dma((IN_FLIGHT + 1,)), s_wkv=dma((2,)), s_wo=dma((n_y,)),
+            s_raw=dma(()), s_rawsend=dma(()), s_rawrecv=dma(()), s_ring=dma((RING,)),
+            s_res=dma(()), s_ress=dma(()), s_resr=dma(()), s_as=dma(()), s_ar=dma((3,)),
+            s_qs=dma(()), s_qr=dma((3, kv_n)),
+            s_xs=dma(()), s_xr=dma((12,)),
+            s_ys=dma(()), s_yr=dma((18,)), s_gs=dma(()), s_gr=dma((3, 2)), s_gl=dma(()),
         )
         hbm = pl.BlockSpec(memory_space=pl.ANY)
         out = pl.pallas_call(

time: 56 us -> 56.2 us (level)
  no operation moved by 1% of the time
where the time goes in v1:
time: 56.2 us; the launch traced here: 56.1 us
  Pallas kernels  56 us (100%)
    pallas_call x1, Pallas kernels, local_step(): pl.pallas_call(functools.partial(kernel, (n_ctx, n_y, kv_n, grp)), out_sh...  55.1 us

profile of v1, /device:TPU:97, one launch (start us, length us, event | category | flops | bytes accessed | tf_op | source)
XLA Modules:
  0.0 56.1 jit_solution(7431276574157674282)
XLA Ops:
  0.0 55.1 %shard_map.100.src = bf16[64,5120]{1,0:T(8,128)(2,1)S(1)} custom-call(bf16[64,5120]{1,0:T(8,128)(2,1)} %hid_h.1, bf16[5120,1024]{1,0:T(8,128)(2,1)} %wq_h.1, bf16[5120,256]{1,0:T(8,128)(2,1)} %wk_h.1, bf16[5120,256]{1,0:T(8,128)(2,1)} %wv_h.1, bf16[1024,5120]{1,0:T(8,128)(2,1)} %wo_h.1, bf16[2048,128]{1,0:T(8,128)(2,1)} %bitcast.6, ...), custom_call_target="tpu_custom_call" | custom-call | tf_op jit(solution)/shard_map/pallas_call | solution.py:560
  55.1 0.8 %shard_map.101 = bf16[64,5120]{1,0:T(8,128)(2,1)} custom-call(bf16[64,5120]{1,0:T(8,128)(2,1)S(1)} %shard_map.100.src), custom_call_target="tpu_custom_call" | custom-call | tf_op jit(solution)/shard_map/pallas_call | solution.py:570

commit v2 on v1

--- a/solution.py
+++ b/solution.py
@@ -348,9 +348,14 @@
         at = pl.ds(0, chunks[chunk][1])
         return remote(ys.at[i, at], yr.at[i, at], s_ys, s_yr.at[i], where)
 
-    def y_post(chunk, val, i, where):
+    def y_post(chunk, val, i, where, now=True):
         ys[i, :val.shape[0]] = val
-        y_copy(chunk, i, where).start()
+        if now:
+            y_copy(chunk, i, where).start()
+
+    def y_near(chunk):
+        y_copy(chunk, 6 * chunk + 2, up).start()
+        y_copy(chunk, 6 * chunk + 3, down).start()
 
     def project(chunk):
         base = 6 * chunk
@@ -368,10 +373,10 @@
         y_post(chunk, one, base, up)
         y_post(chunk, two, base + 1, down)
         one, two = y_part(1)
-        y_post(chunk, two, base + 2, up)
+        y_post(chunk, two, base + 2, up, chunk == 0)
         yhold[chunk, 0, :n] = one
         one, two = y_part(n_y - 1)
-        y_post(chunk, one, base + 3, down)
+        y_post(chunk, one, base + 3, down, chunk == 0)
         yhold[chunk, 1, :n] = two
         one, two = y_part(0)
         yhold[chunk, 2, :n] = one
@@ -462,19 +467,20 @@
     suffix_group(1)
     relay(0)
     relay(1)
-    suffix_group(2)
+    for group in range(2, n_groups):
+        suffix_group(group)
     merge_prefix(0)
     combine(0)
+    merge_prefix(1)
+    combine(1)
     wait(c_res)
-    merge_prefix(1)
     project(0)
-    for group in range(3, n_groups):
-        suffix_group(group)
-    combine(1)
     combine(2)
-    y_relay(0)
     project(1)
     project(2)
+    y_relay(0)
+    y_near(1)
+    y_near(2)
     y_relay(1)
     y_relay(2)
     finish(0)

time: 56.2 us -> 55 us (0.979)
  Pallas kernels: 56 us -> 54.7 us
    pallas_call x1, Pallas kernels: 55.1 us -> 53.9 us  [local_step(): pl.pallas_call(functools.partial(kernel, (n_ctx, n_y, kv_n, grp)), out_sh...]
where the time goes in v2:
time: 55 us; the launch traced here: 54.9 us
  Pallas kernels  54.7 us (99%)
    pallas_call x1, Pallas kernels, local_step(): pl.pallas_call(functools.partial(kernel, (n_ctx, n_y, kv_n, grp)), out_sh...  53.9 us

profile of v2, /device:TPU:97, one launch (start us, length us, event | category | flops | bytes accessed | tf_op | source)
XLA Modules:
  0.0 54.9 jit_solution(15312758711317796904)
XLA Ops:
  0.0 53.9 %shard_map.100.src = bf16[64,5120]{1,0:T(8,128)(2,1)S(1)} custom-call(bf16[64,5120]{1,0:T(8,128)(2,1)} %hid_h.1, bf16[5120,1024]{1,0:T(8,128)(2,1)} %wq_h.1, bf16[5120,256]{1,0:T(8,128)(2,1)} %wk_h.1, bf16[5120,256]{1,0:T(8,128)(2,1)} %wv_h.1, bf16[1024,5120]{1,0:T(8,128)(2,1)} %wo_h.1, bf16[2048,128]{1,0:T(8,128)(2,1)} %bitcast.6, ...), custom_call_target="tpu_custom_call" | custom-call | tf_op jit(solution)/shard_map/pallas_call | solution.py:566
  53.9 0.8 %shard_map.101 = bf16[64,5120]{1,0:T(8,128)(2,1)} custom-call(bf16[64,5120]{1,0:T(8,128)(2,1)S(1)} %shard_map.100.src), custom_call_target="tpu_custom_call" | custom-call | tf_op jit(solution)/shard_map/pallas_call | solution.py:576

commit v3 on v2

--- a/solution.py
+++ b/solution.py
@@ -14,8 +14,9 @@
 GROUP = 16
 RING = 2
 POS_CHUNK = 512
-PIECES = 5
-IN_FLIGHT = 6
+PIECES = 2
+SPLIT = 4
+IN_FLIGHT = 2
 VMEM_BYTES = 66000000
 
 
@@ -86,9 +87,13 @@
     c_hid = pltpu.make_async_copy(hid_h, hid, s_hid)
     c_raw = [pltpu.make_async_copy(src, raw.at[0, i], s_raw) for i, src in enumerate((pk_h, pv_h))]
     deep = width // PIECES
-    c_wq = [pltpu.make_async_copy(wq_h.at[pl.ds(k * deep, deep), pl.ds(kv * grp * head, grp * head)],
-                                  wq.at[kv, pl.ds(k * deep, deep), :], s_wq.at[(kv * PIECES + k) % (IN_FLIGHT + 1)])
-            for kv in range(kv_n) for k in range(PIECES)]
+    fine = deep // SPLIT
+
+    def wq_copies(kv, k):
+        cols = pl.ds(kv * grp * head, grp * head)
+        return [pltpu.make_async_copy(wq_h.at[pl.ds(k * deep + j * fine, fine), cols],
+                                      wq.at[kv, pl.ds(k * deep + j * fine, fine), :], s_wq.at[kv, k]) for j in range(SPLIT)]
+
     c_wkv = [pltpu.make_async_copy(src, dst, s_wkv.at[i]) for i, (src, dst) in enumerate(((wk_h, wk), (wv_h, wv)))]
     c_wo = []
     for r in range(n_y):
@@ -109,11 +114,11 @@
         for c in copies:
             c.wait()
 
-    queue = c_wq + c_raw + c_wkv
+    queue = [wq_copies(kv, k) for kv in range(kv_n) for k in range(PIECES)] + [c_raw] + [[c] for c in c_wkv]
 
     def advance():
         if queue:
-            queue.pop(0).start()
+            start(queue.pop(0))
 
     c_hid.start()
     for _ in range(IN_FLIGHT):
@@ -132,9 +137,9 @@
     def queries(kv):
         total = None
         for k in range(PIECES):
-            c_wq[kv * PIECES + k].wait()
+            at = pl.ds(k * deep, deep)
+            pltpu.make_async_copy(wq.at[kv, at, :], wq.at[kv, at, :], s_wq.at[kv, k]).wait()
             advance()
-            at = pl.ds(k * deep, deep)
             term = dot_nn(hid[:, at], wq[kv, at, :])
             total = term if total is None else total + term
         part = total.astype(BF16)
@@ -252,13 +257,13 @@
         for i, state in enumerate(prefix_states([(both, 0), (both, 1)])):
             keep(own, i, state)
 
-    def relay(chunk):
-        base = 6 * chunk
-        for i, where in ((base + 2, right), (base + 3, left)):
-            x_copies(i, where).wait_recv()
-        to_right, to_left = (merge(arrived(base + 2 + i), kept(hold, 2 * chunk + i)) for i in range(2))
-        post(to_right, base + 4, right)
-        post(to_left, base + 5, left)
+    def relay():
+        for base in (0, 6):
+            for i, where in ((base + 2, right), (base + 3, left)):
+                x_copies(i, where).wait_recv()
+        ready = [merge(arrived(6 * (n // 2) + 2 + n % 2), kept(hold, n)) for n in range(4)]
+        for n in range(4):
+            post(ready[n], 6 * (n // 2) + 4 + n % 2, (right, left)[n % 2])
 
     lines = GROUP * heads
     span = ring.shape[3]
@@ -465,8 +470,7 @@
 
     suffix_group(0)
     suffix_group(1)
-    relay(0)
-    relay(1)
+    relay()
     for group in range(2, n_groups):
         suffix_group(group)
     merge_prefix(0)
@@ -555,7 +559,7 @@
             ys=pltpu.VMEM((18, half_rows, blk // 2), F32),
             yr=pltpu.VMEM((18, half_rows, blk // 2), F32),
             yblk=pltpu.VMEM((3, 2, half_rows, blk // 2), BF16),
-            s_hid=dma(()), s_wq=dma((IN_FLIGHT + 1,)), s_wkv=dma((2,)), s_wo=dma((n_y,)),
+            s_hid=dma(()), s_wq=dma((kv_n, PIECES)), s_wkv=dma((2,)), s_wo=dma((n_y,)),
             s_raw=dma(()), s_rawsend=dma(()), s_rawrecv=dma(()), s_ring=dma((RING,)),
             s_res=dma(()), s_ress=dma(()), s_resr=dma(()), s_as=dma(()), s_ar=dma((3,)),
             s_qs=dma(()), s_qr=dma((3, kv_n)),

time: 55 us -> 55.5 us (level)
  Pallas kernels: 54.7 us -> 55.3 us
where the time goes in v3:
time: 55.5 us; the launch traced here: 55.4 us
  Pallas kernels  55.3 us (100%)
    pallas_call x1, Pallas kernels, local_step(): pl.pallas_call(functools.partial(kernel, (n_ctx, n_y, kv_n, grp)), out_sh...  54.4 us

profile of v3, /device:TPU:97, one launch (start us, length us, event | category | flops | bytes accessed | tf_op | source)
XLA Modules:
  0.0 55.4 jit_solution(18285092560504674929)
XLA Ops:
  0.0 54.4 %shard_map.100.src = bf16[64,5120]{1,0:T(8,128)(2,1)S(1)} custom-call(bf16[64,5120]{1,0:T(8,128)(2,1)} %hid_h.1, bf16[5120,1024]{1,0:T(8,128)(2,1)} %wq_h.1, bf16[5120,256]{1,0:T(8,128)(2,1)} %wk_h.1, bf16[5120,256]{1,0:T(8,128)(2,1)} %wv_h.1, bf16[1024,5120]{1,0:T(8,128)(2,1)} %wo_h.1, bf16[2048,128]{1,0:T(8,128)(2,1)} %bitcast.6, ...), custom_call_target="tpu_custom_call" | custom-call | tf_op jit(solution)/shard_map/pallas_call | solution.py:570
  54.4 0.8 %shard_map.101 = bf16[64,5120]{1,0:T(8,128)(2,1)} custom-call(bf16[64,5120]{1,0:T(8,128)(2,1)S(1)} %shard_map.100.src), custom_call_target="tpu_custom_call" | custom-call | tf_op jit(solution)/shard_map/pallas_call | solution.py:580
